TPU v7x, 32 devices: a whole 2x2x4 slice. The times are simulated.
32 devices in a mesh: row: 8 (over y, x, core), col: 4 (over z).
Axes of the slice: x: 2, y: 2, z: 4, core: 2. Of those that a mesh axis runs over, the one named last changes fastest.
Arguments:
- blocks: bfloat16 [8, 4, 368, 128, 128], P('row', 'col'), may hold values from -0.125 to 0.125
- block_rows: int32 [8, 4, 368], P('row', 'col'), may hold values from 0 to 31, as said below
- block_cols: int32 [8, 4, 368], P('row', 'col'), may hold values from 0 to 63
- counts: int32 [8, 4], P('row', 'col'), may hold values from 1 to 368, as said below
- features: bfloat16 [32768, 256], P(('col', 'row')), may hold values from -6 to 6
Outputs:
- aggregated: bfloat16 [32768, 256], P(('row', 'col'))
Inputs may be any that keep to these rules, and one draw needn't show every extreme that they name: `block_rows`: within one tile the live slots name distinct pairs of block row and block column. `counts`: some tile holds exactly 368 live blocks in every draw.
All inputs are finite; a program needn't handle non-finite values.
Results may differ from a plain program's by a relative error of at most 0.013.
Values may be sent and summed in bfloat16 or wider, within the bound.
A program may use at most 128 MiB of HBM per device.

v0:
```python
import jax
import jax.numpy as jnp
from jax import lax
from jax.sharding import PartitionSpec as P


def on_device(blocks, block_rows, block_cols, counts, features):
    feature_width = features.shape[1]
    block_size = blocks.shape[-1]
    max_blocks = blocks.shape[2]
    group_size = max_blocks // 8
    row_blocks = lax.axis_size("col") * (features.shape[0] // block_size)
    panel_rows = lax.all_gather(features, "row", axis=0, tiled=True)
    panel_blocks = panel_rows.reshape(-1, block_size, feature_width)
    tile_blocks = blocks[0, 0]
    tile_rows = block_rows[0, 0]
    tile_cols = block_cols[0, 0]
    live_count = counts[0, 0]

    def accumulate(group_index, running):
        first_slot = group_index * group_size
        weights = lax.dynamic_slice_in_dim(tile_blocks, first_slot, group_size, 0)
        rows_slice = lax.dynamic_slice_in_dim(tile_rows, first_slot, group_size, 0)
        cols_slice = lax.dynamic_slice_in_dim(tile_cols, first_slot, group_size, 0)
        positions = first_slot + jnp.arange(group_size, dtype=jnp.int32)
        weights = jnp.where(
            (positions < live_count)[:, None, None], weights, jnp.zeros_like(weights)
        )
        gathered = panel_blocks[cols_slice, :, 0:feature_width]
        product = jnp.einsum("gik,gkf->gif", weights, gathered, preferred_element_type=jnp.float32)
        return running.at[rows_slice].add(product)

    initial = jnp.zeros((row_blocks, block_size, feature_width - 0), jnp.float32)
    groups = 8
    running = lax.fori_loop(0, groups, accumulate, initial)
    return lax.psum_scatter(
        running.reshape(row_blocks * block_size, feature_width - 0).astype(jnp.bfloat16),
        "col",
        scatter_dimension=0,
        tiled=True,
    )


def solution(mesh):
    return jax.shard_map(
        on_device,
        mesh=mesh,
        in_specs=(
            P("row", "col", None, None, None),
            P("row", "col", None),
            P("row", "col", None),
            P("row", "col"),
            P(("col", "row"), None),
        ),
        out_specs=P(("row", "col"), None),
        check_vma=False,
    )
```

profile of v0, /device:TPU:0, one launch (start us, length us, event | category | flops | bytes accessed | tf_op | source)
XLA Modules:
  0.0 290.6 jit_solution(15859293063505907300)
XLA Ops:
  6.5 0.0 all-gather.2.cloned.1.call-start
  6.5 0.7 all-gather.2.cloned.1.call-update
  7.3 0.0 reduce-scatter.2.cloned.1.call-start
  7.3 0.7 reduce
  8.0 0.7 reduce.1
  8.7 39.9 %all-gather.2.cloned.1.call-done = bf16[8192,256]{1,0:T(8,128)(2,1)} async-done(((bf16[1024,256]{1,0:T(8,128)(2,1)}), bf16[8192,256]{1,0:T(8,128)(2,1)}) %all-gather.2.cloned.1.call-update) | async-done | bytes 4194320 | tf_op jit(solution)/shard_map/all_gather | solution.py:13
  48.6 2.6 broadcast_in_dim.38
  51.1 185.2 %while.13 = (s32[]{:T(128)}, f32[32,128,256]{2,1,0:T(8,128)}, s32[368]{0:T(512)S(1)}, s32[]{:T(128)}, bf16[368,128,128]{2,1,0:T(8,128)(2,1)}, /*index=5*/s32[368...) while((s32[]{:T(128)}, f32[32,128,256]{2,1,0:T(8,128)}, ...), condition=%wide.region_2.3_spmd, body=%wide.region_0.2_spmd.sunk | while | flops 388138368 | bytes 34674192 | solution.py:35
  51.1 0.7 add_compare_fusion.2
  51.8 0.1 compare_select_fusion.3
  51.9 2.9 %gather_fusion = bf16[46,128,256]{2,1,0:T(8,128)(2,1)S(1)} fusion(bf16[64,128,256]{2,1,0:T(8,128)(2,1)} %get-tuple-element.221, s32[1024]{0:T(1024)S(1)} %pad_clamp_fusion.2), kind=kCustom, calls=%fused_computation.clone.1 | custom fusion | bytes 6029496 | tf_op jit(solution)/shard_map/while/body/eval_jaxpr/gather | solution.py:29
  54.8 5.0 %fusion.13 = f32[46,128,256]{2,1,0:T(8,128)} fusion(bf16[46,128,256]{2,1,0:T(8,128)(2,1)S(1)} %gather_fusion, bf16[368,128,128]{2,1,0:T(8,128)(2,1)} %get-tuple-element.219, s32[]{:T(128)S(6)} %select_n.40, pred[46]{0:T(512)(128)(4,1)S(1)} %add_compare_fusion.2), kind=kOutput, calls=%fused_computation.2.clone.1 | convolution fusion | flops 386629632 | bytes 10551346 | tf_op jit(solution)/shard_map/while/body/eval_jaxpr/gik,gkf->gif/dot_general | solution.py:30
  59.8 14.4 %scatter_fusion = f32[32,128,256]{2,1,0:T(8,128)} fusion(f32[32,128,256]{2,1,0:T(8,128)} %get-tuple-element.205, s32[46]{0:T(128)S(1)} %get-tuple-element.191, f32[46,128,256]{2,1,0:T(8,128)} %fusion.13), kind=kCustom, calls=%fused_computation.1.clone.1 | custom fusion | flops 1507328 | bytes 18088120 | tf_op jit(solution)/shard_map/while/body/eval_jaxpr/scatter-add | solution.py:31
  74.1 0.7 add_compare_fusion.2
  74.8 0.1 compare_select_fusion.3
  74.9 2.9 %gather_fusion = bf16[46,128,256]{2,1,0:T(8,128)(2,1)S(1)} fusion(bf16[64,128,256]{2,1,0:T(8,128)(2,1)} %get-tuple-element.221, s32[1024]{0:T(1024)S(1)} %pad_clamp_fusion.2), kind=kCustom, calls=%fused_computation.clone.1 | custom fusion | bytes 6029496 | tf_op jit(solution)/shard_map/while/body/eval_jaxpr/gather | solution.py:29
  77.8 5.0 %fusion.13 = f32[46,128,256]{2,1,0:T(8,128)} fusion(bf16[46,128,256]{2,1,0:T(8,128)(2,1)S(1)} %gather_fusion, bf16[368,128,128]{2,1,0:T(8,128)(2,1)} %get-tuple-element.219, s32[]{:T(128)S(6)} %select_n.40, pred[46]{0:T(512)(128)(4,1)S(1)} %add_compare_fusion.2), kind=kOutput, calls=%fused_computation.2.clone.1 | convolution fusion | flops 386629632 | bytes 10551346 | tf_op jit(solution)/shard_map/while/body/eval_jaxpr/gik,gkf->gif/dot_general | solution.py:30
  82.8 14.5 %scatter_fusion = f32[32,128,256]{2,1,0:T(8,128)} fusion(f32[32,128,256]{2,1,0:T(8,128)} %get-tuple-element.205, s32[46]{0:T(128)S(1)} %get-tuple-element.191, f32[46,128,256]{2,1,0:T(8,128)} %fusion.13), kind=kCustom, calls=%fused_computation.1.clone.1 | custom fusion | flops 1507328 | bytes 18088120 | tf_op jit(solution)/shard_map/while/body/eval_jaxpr/scatter-add | solution.py:31
  97.2 0.7 add_compare_fusion.2
  97.9 0.1 compare_select_fusion.3
  98.0 2.9 %gather_fusion = bf16[46,128,256]{2,1,0:T(8,128)(2,1)S(1)} fusion(bf16[64,128,256]{2,1,0:T(8,128)(2,1)} %get-tuple-element.221, s32[1024]{0:T(1024)S(1)} %pad_clamp_fusion.2), kind=kCustom, calls=%fused_computation.clone.1 | custom fusion | bytes 6029496 | tf_op jit(solution)/shard_map/while/body/eval_jaxpr/gather | solution.py:29
  100.9 5.0 %fusion.13 = f32[46,128,256]{2,1,0:T(8,128)} fusion(bf16[46,128,256]{2,1,0:T(8,128)(2,1)S(1)} %gather_fusion, bf16[368,128,128]{2,1,0:T(8,128)(2,1)} %get-tuple-element.219, s32[]{:T(128)S(6)} %select_n.40, pred[46]{0:T(512)(128)(4,1)S(1)} %add_compare_fusion.2), kind=kOutput, calls=%fused_computation.2.clone.1 | convolution fusion | flops 386629632 | bytes 10551346 | tf_op jit(solution)/shard_map/while/body/eval_jaxpr/gik,gkf->gif/dot_general | solution.py:30
  105.9 14.5 %scatter_fusion = f32[32,128,256]{2,1,0:T(8,128)} fusion(f32[32,128,256]{2,1,0:T(8,128)} %get-tuple-element.205, s32[46]{0:T(128)S(1)} %get-tuple-element.191, f32[46,128,256]{2,1,0:T(8,128)} %fusion.13), kind=kCustom, calls=%fused_computation.1.clone.1 | custom fusion | flops 1507328 | bytes 18088120 | tf_op jit(solution)/shard_map/while/body/eval_jaxpr/scatter-add | solution.py:31
  120.4 0.7 add_compare_fusion.2
  121.0 0.1 compare_select_fusion.3
  121.1 2.9 %gather_fusion = bf16[46,128,256]{2,1,0:T(8,128)(2,1)S(1)} fusion(bf16[64,128,256]{2,1,0:T(8,128)(2,1)} %get-tuple-element.221, s32[1024]{0:T(1024)S(1)} %pad_clamp_fusion.2), kind=kCustom, calls=%fused_computation.clone.1 | custom fusion | bytes 6029496 | tf_op jit(solution)/shard_map/while/body/eval_jaxpr/gather | solution.py:29
  124.0 5.0 %fusion.13 = f32[46,128,256]{2,1,0:T(8,128)} fusion(bf16[46,128,256]{2,1,0:T(8,128)(2,1)S(1)} %gather_fusion, bf16[368,128,128]{2,1,0:T(8,128)(2,1)} %get-tuple-element.219, s32[]{:T(128)S(6)} %select_n.40, pred[46]{0:T(512)(128)(4,1)S(1)} %add_compare_fusion.2), kind=kOutput, calls=%fused_computation.2.clone.1 | convolution fusion | flops 386629632 | bytes 10551346 | tf_op jit(solution)/shard_map/while/body/eval_jaxpr/gik,gkf->gif/dot_general | solution.py:30
  129.0 14.3 %scatter_fusion = f32[32,128,256]{2,1,0:T(8,128)} fusion(f32[32,128,256]{2,1,0:T(8,128)} %get-tuple-element.205, s32[46]{0:T(128)S(1)} %get-tuple-element.191, f32[46,128,256]{2,1,0:T(8,128)} %fusion.13), kind=kCustom, calls=%fused_computation.1.clone.1 | custom fusion | flops 1507328 | bytes 18088120 | tf_op jit(solution)/shard_map/while/body/eval_jaxpr/scatter-add | solution.py:31
  143.3 0.7 add_compare_fusion.2
  143.9 0.1 compare_select_fusion.3
  144.0 2.9 %gather_fusion = bf16[46,128,256]{2,1,0:T(8,128)(2,1)S(1)} fusion(bf16[64,128,256]{2,1,0:T(8,128)(2,1)} %get-tuple-element.221, s32[1024]{0:T(1024)S(1)} %pad_clamp_fusion.2), kind=kCustom, calls=%fused_computation.clone.1 | custom fusion | bytes 6029496 | tf_op jit(solution)/shard_map/while/body/eval_jaxpr/gather | solution.py:29
  147.0 5.0 %fusion.13 = f32[46,128,256]{2,1,0:T(8,128)} fusion(bf16[46,128,256]{2,1,0:T(8,128)(2,1)S(1)} %gather_fusion, bf16[368,128,128]{2,1,0:T(8,128)(2,1)} %get-tuple-element.219, s32[]{:T(128)S(6)} %select_n.40, pred[46]{0:T(512)(128)(4,1)S(1)} %add_compare_fusion.2), kind=kOutput, calls=%fused_computation.2.clone.1 | convolution fusion | flops 386629632 | bytes 10551346 | tf_op jit(solution)/shard_map/while/body/eval_jaxpr/gik,gkf->gif/dot_general | solution.py:30
  151.9 14.6 %scatter_fusion = f32[32,128,256]{2,1,0:T(8,128)} fusion(f32[32,128,256]{2,1,0:T(8,128)} %get-tuple-element.205, s32[46]{0:T(128)S(1)} %get-tuple-element.191, f32[46,128,256]{2,1,0:T(8,128)} %fusion.13), kind=kCustom, calls=%fused_computation.1.clone.1 | custom fusion | flops 1507328 | bytes 18088120 | tf_op jit(solution)/shard_map/while/body/eval_jaxpr/scatter-add | solution.py:31
  166.5 0.7 add_compare_fusion.2
  167.2 0.1 compare_select_fusion.3
  167.3 2.9 %gather_fusion = bf16[46,128,256]{2,1,0:T(8,128)(2,1)S(1)} fusion(bf16[64,128,256]{2,1,0:T(8,128)(2,1)} %get-tuple-element.221, s32[1024]{0:T(1024)S(1)} %pad_clamp_fusion.2), kind=kCustom, calls=%fused_computation.clone.1 | custom fusion | bytes 6029496 | tf_op jit(solution)/shard_map/while/body/eval_jaxpr/gather | solution.py:29
  170.2 5.0 %fusion.13 = f32[46,128,256]{2,1,0:T(8,128)} fusion(bf16[46,128,256]{2,1,0:T(8,128)(2,1)S(1)} %gather_fusion, bf16[368,128,128]{2,1,0:T(8,128)(2,1)} %get-tuple-element.219, s32[]{:T(128)S(6)} %select_n.40, pred[46]{0:T(512)(128)(4,1)S(1)} %add_compare_fusion.2), kind=kOutput, calls=%fused_computation.2.clone.1 | convolution fusion | flops 386629632 | bytes 10551346 | tf_op jit(solution)/shard_map/while/body/eval_jaxpr/gik,gkf->gif/dot_general | solution.py:30
  175.2 14.6 %scatter_fusion = f32[32,128,256]{2,1,0:T(8,128)} fusion(f32[32,128,256]{2,1,0:T(8,128)} %get-tuple-element.205, s32[46]{0:T(128)S(1)} %get-tuple-element.191, f32[46,128,256]{2,1,0:T(8,128)} %fusion.13), kind=kCustom, calls=%fused_computation.1.clone.1 | custom fusion | flops 1507328 | bytes 18088120 | tf_op jit(solution)/shard_map/while/body/eval_jaxpr/scatter-add | solution.py:31
  189.8 0.7 add_compare_fusion.2
  190.5 0.1 compare_select_fusion.3
  190.6 2.9 %gather_fusion = bf16[46,128,256]{2,1,0:T(8,128)(2,1)S(1)} fusion(bf16[64,128,256]{2,1,0:T(8,128)(2,1)} %get-tuple-element.221, s32[1024]{0:T(1024)S(1)} %pad_clamp_fusion.2), kind=kCustom, calls=%fused_computation.clone.1 | custom fusion | bytes 6029496 | tf_op jit(solution)/shard_map/while/body/eval_jaxpr/gather | solution.py:29
  193.5 5.0 %fusion.13 = f32[46,128,256]{2,1,0:T(8,128)} fusion(bf16[46,128,256]{2,1,0:T(8,128)(2,1)S(1)} %gather_fusion, bf16[368,128,128]{2,1,0:T(8,128)(2,1)} %get-tuple-element.219, s32[]{:T(128)S(6)} %select_n.40, pred[46]{0:T(512)(128)(4,1)S(1)} %add_compare_fusion.2), kind=kOutput, calls=%fused_computation.2.clone.1 | convolution fusion | flops 386629632 | bytes 10551346 | tf_op jit(solution)/shard_map/while/body/eval_jaxpr/gik,gkf->gif/dot_general | solution.py:30
  198.5 14.6 %scatter_fusion = f32[32,128,256]{2,1,0:T(8,128)} fusion(f32[32,128,256]{2,1,0:T(8,128)} %get-tuple-element.205, s32[46]{0:T(128)S(1)} %get-tuple-element.191, f32[46,128,256]{2,1,0:T(8,128)} %fusion.13), kind=kCustom, calls=%fused_computation.1.clone.1 | custom fusion | flops 1507328 | bytes 18088120 | tf_op jit(solution)/shard_map/while/body/eval_jaxpr/scatter-add | solution.py:31
  213.1 0.7 add_compare_fusion.2
  213.8 0.1 compare_select_fusion.3
  213.8 2.9 %gather_fusion = bf16[46,128,256]{2,1,0:T(8,128)(2,1)S(1)} fusion(bf16[64,128,256]{2,1,0:T(8,128)(2,1)} %get-tuple-element.221, s32[1024]{0:T(1024)S(1)} %pad_clamp_fusion.2), kind=kCustom, calls=%fused_computation.clone.1 | custom fusion | bytes 6029496 | tf_op jit(solution)/shard_map/while/body/eval_jaxpr/gather | solution.py:29
  216.8 5.0 %fusion.13 = f32[46,128,256]{2,1,0:T(8,128)} fusion(bf16[46,128,256]{2,1,0:T(8,128)(2,1)S(1)} %gather_fusion, bf16[368,128,128]{2,1,0:T(8,128)(2,1)} %get-tuple-element.219, s32[]{:T(128)S(6)} %select_n.40, pred[46]{0:T(512)(128)(4,1)S(1)} %add_compare_fusion.2), kind=kOutput, calls=%fused_computation.2.clone.1 | convolution fusion | flops 386629632 | bytes 10551346 | tf_op jit(solution)/shard_map/while/body/eval_jaxpr/gik,gkf->gif/dot_general | solution.py:30
  221.7 14.6 %scatter_fusion = f32[32,128,256]{2,1,0:T(8,128)} fusion(f32[32,128,256]{2,1,0:T(8,128)} %get-tuple-element.205, s32[46]{0:T(128)S(1)} %get-tuple-element.191, f32[46,128,256]{2,1,0:T(8,128)} %fusion.13), kind=kCustom, calls=%fused_computation.1.clone.1 | custom fusion | flops 1507328 | bytes 18088120 | tf_op jit(solution)/shard_map/while/body/eval_jaxpr/scatter-add | solution.py:31
  236.3 3.8 %convert_element_type.6 = bf16[32,128,256]{2,1,0:T(8,128)(2,1)} convert(f32[32,128,256]{2,1,0:T(8,128)} %get-tuple-element.129) | non-fusion elementwise | flops 1048576 | bytes 6291456 | tf_op jit(solution)/shard_map/convert_element_type | solution.py:37
  240.1 0.0 reduce-scatter.2.cloned.1.call-update
  240.1 43.6 %reduce-scatter.2.cloned.1.call-done = bf16[1024,256]{1,0:T(8,128)(2,1)} async-done(((bf16[4096,256]{1,0:T(8,128)(2,1)}), bf16[1024,256]{1,0:T(8,128)(2,1)}) %reduce-scatter.2.cloned.1.call-update) | async-done | bytes 524304 | tf_op jit(solution)/shard_map/reduce_scatter | solution.py:36
  (8 shorter events, 0.1 us)
Async XLA Ops:
  6.5 42.0 %all-gather.2.cloned.1.call-start = ((), (), s32[]{:S(2)}) async-start(), calls=%async_computation.1 | async-start | bytes 4718592 | tf_op jit(solution)/shard_map/all_gather | solution.py:13
  7.3 276.5 %reduce-scatter.2.cloned.1.call-start = ((), (), s32[]{:S(2)}) async-start(), calls=%async_computation.2 | async-start | bytes 2621440 | tf_op jit(solution)/shard_map/reduce_scatter | solution.py:36
Sparse Core Ops, SparseCore 0:
  9.2 39.2 all-gather.1
  240.3 43.4 reduce-scatter.1
where the time goes:
time: 292 us; the launch traced here: 291 us
  other arithmetic  127 us (43%)
  waiting for transfers between devices  84.2 us (29%)
  matrix products  39.7 us (14%)
  local copies, waits for them, and re-layouts  26 us (9%)
  between operations  13.4 us (5%)
    scatter-add x8, other arithmetic, accumulate(): return running.at[rows_slice].add(product)  116 us
    reduce_scatter x1, waiting for transfers between devices, on_device(): lax.psum_scatter(running.reshape(row_blocks * block_size, feature_width -...  43.6 us
    all_gather x1, waiting for transfers between devices, on_device(): panel_rows = lax.all_gather(features, 'row', axis=0, tiled=True)  39.9 us
    dot_general x8, matrix products, accumulate(): jnp.einsum('gik,gkf->gif', weights, gathered, preferred_element_type=jnp....  39.7 us
    gather x8, local copies, waits for them, and re-layouts, accumulate(): gathered = panel_blocks[cols_slice, :, 0:feature_width]  23.4 us
  transfers between devices with their start and end apart: 2, of which 2 were waited for; matrix products, arithmetic and copies ran while one was open for 0% of the time, Pallas kernels for 0%

commit v1 on v0

--- a/solution.py
+++ b/solution.py
@@ -10,7 +10,9 @@
     max_blocks = blocks.shape[2]
     group_size = max_blocks // 8
     row_blocks = lax.axis_size("col") * (features.shape[0] // block_size)
-    panel_rows = lax.all_gather(features, "row", axis=0, tiled=True)
+    panel_rows = jnp.concatenate(
+        lax.all_to_all(jnp.stack([features] * lax.axis_size("row")), "row", 0, 0), axis=0
+    )
     panel_blocks = panel_rows.reshape(-1, block_size, feature_width)
     tile_blocks = blocks[0, 0]
     tile_rows = block_rows[0, 0]

time: 292 us -> 308 us (1.055)
  waiting for transfers between devices: 84.2 us -> 92.7 us
  starting transfers between devices: 0.04 us -> 5.37 us
  local copies, waits for them, and re-layouts: 26 us -> 29.2 us
    all_to_all x0 -> x1, waiting for transfers between devices: none -> 49.1 us  [on_device(): lax.all_to_all(jnp.stack([features] * lax.axis_size('row')), 'row', 0, 0)]
    all_gather x1 -> x0, waiting for transfers between devices: 39.9 us -> none  [on_device(): panel_rows = lax.all_gather(features, 'row', axis=0, tiled=True)]
    all_to_all x0 -> x1, starting transfers between devices: none -> 5.33 us  [on_device(): lax.all_to_all(jnp.stack([features] * lax.axis_size('row')), 'row', 0, 0)]
    another operation x0 -> x1, local copies, waits for them, and re-layouts: none -> 3.24 us  [on_device(): jnp.stack([features] * lax.axis_size('row'))]
where the time goes in v1:
time: 308 us; the launch traced here: 306 us
  other arithmetic  126 us (41%)
  waiting for transfers between devices  92.7 us (30%)
  matrix products  39.7 us (13%)
  local copies, waits for them, and re-layouts  29.2 us (9%)
  between operations  13.4 us (4%)
  starting transfers between devices  5.37 us (2%)
    scatter-add x8, other arithmetic, accumulate(): return running.at[rows_slice].add(product)  116 us
    all_to_all x1, waiting for transfers between devices, on_device(): lax.all_to_all(jnp.stack([features] * lax.axis_size('row')), 'row', 0, 0)  49.1 us
    reduce_scatter x1, waiting for transfers between devices, on_device(): lax.psum_scatter(running.reshape(row_blocks * block_size, feature_width -...  43.6 us
    dot_general x8, matrix products, accumulate(): jnp.einsum('gik,gkf->gif', weights, gathered, preferred_element_type=jnp....  39.7 us
    gather x8, local copies, waits for them, and re-layouts, accumulate(): gathered = panel_blocks[cols_slice, :, 0:feature_width]  23.4 us
  transfers between devices with their start and end apart: 2, of which 2 were waited for; matrix products, arithmetic and copies ran while one was open for 0% of the time, Pallas kernels for 0%

profile of v1, /device:TPU:0, one launch (start us, length us, event | category | flops | bytes accessed | tf_op | source)
XLA Modules:
  0.0 306.4 jit_solution(10011990817115027331)
XLA Ops:
  6.5 3.2 %stack.2 = bf16[8,1024,256]{2,1,0:T(8,128)(2,1)} broadcast(bf16[1024,256]{1,0:T(8,128)(2,1)} %param.11), dimensions={1,2} | broadcast | bytes 4718592 | tf_op jit(solution)/shard_map/stack | solution.py:14
  9.8 0.0 copy-start
  9.8 0.0 copy-start.1
  9.8 5.3 %all-to-all-start = ((bf16[8,1024,256]{2,1,0:T(8,128)(2,1)}), bf16[8,1024,256]{2,1,0:T(8,128)(2,1)}, u32[]{:S(2)}, u32[]{:S(2)}) async-start(bf16[8,1024,256]{2,1,0:T(8,128)(2,1)} %stack.2), calls=%async_computation | async-start | bytes 8388608 | tf_op jit(solution)/shard_map/all_to_all | solution.py:14
  15.1 0.0 reduce-scatter.2.cloned.1.call-start
  15.1 0.0 copy-done
  15.2 0.0 copy-done.1
  15.2 49.1 %all-to-all-done = bf16[8,1024,256]{2,1,0:T(8,128)(2,1)} async-done(((bf16[8,1024,256]{2,1,0:T(8,128)(2,1)}), bf16[8,1024,256]{2,1,0:T(8,128)(2,1)}, u32[]{:S(2)}, u32[]{:S(2)}) %all-to-all-start) | async-done | bytes 4194336 | tf_op jit(solution)/shard_map/all_to_all | solution.py:14
  64.3 2.6 broadcast_in_dim.38
  66.9 185.2 %while.13 = (s32[]{:T(128)}, f32[32,128,256]{2,1,0:T(8,128)}, s32[368]{0:T(512)S(1)}, s32[]{:T(128)}, bf16[368,128,128]{2,1,0:T(8,128)(2,1)}, /*index=5*/s32[368...) while((s32[]{:T(128)}, f32[32,128,256]{2,1,0:T(8,128)}, ...), condition=%wide.region_2.3_spmd, body=%wide.region_0.2_spmd.sunk | while | flops 388138368 | bytes 34674192 | solution.py:37
  66.9 0.7 add_compare_fusion.2
  67.5 0.1 compare_select_fusion.3
  67.6 2.9 gather_fusion
  70.5 5.0 %fusion.13 = f32[46,128,256]{2,1,0:T(8,128)} fusion(bf16[46,128,256]{2,1,0:T(8,128)(2,1)S(1)} %gather_fusion, bf16[368,128,128]{2,1,0:T(8,128)(2,1)} %get-tuple-element.219, s32[]{:T(128)S(6)} %select_n.40, pred[46]{0:T(512)(128)(4,1)S(1)} %add_compare_fusion.2), kind=kOutput, calls=%fused_computation.2.clone.1 | convolution fusion | flops 386629632 | bytes 10551346 | tf_op jit(solution)/shard_map/while/body/eval_jaxpr/gik,gkf->gif/dot_general | solution.py:32
  75.5 14.4 %scatter_fusion = f32[32,128,256]{2,1,0:T(8,128)} fusion(f32[32,128,256]{2,1,0:T(8,128)} %get-tuple-element.205, s32[46]{0:T(128)S(1)} %get-tuple-element.191, f32[46,128,256]{2,1,0:T(8,128)} %fusion.13), kind=kCustom, calls=%fused_computation.1.clone.1 | custom fusion | flops 1507328 | bytes 18088120 | tf_op jit(solution)/shard_map/while/body/eval_jaxpr/scatter-add | solution.py:33
  89.9 0.7 add_compare_fusion.2
  90.5 0.1 compare_select_fusion.3
  90.6 2.9 gather_fusion
  93.5 5.0 %fusion.13 = f32[46,128,256]{2,1,0:T(8,128)} fusion(bf16[46,128,256]{2,1,0:T(8,128)(2,1)S(1)} %gather_fusion, bf16[368,128,128]{2,1,0:T(8,128)(2,1)} %get-tuple-element.219, s32[]{:T(128)S(6)} %select_n.40, pred[46]{0:T(512)(128)(4,1)S(1)} %add_compare_fusion.2), kind=kOutput, calls=%fused_computation.2.clone.1 | convolution fusion | flops 386629632 | bytes 10551346 | tf_op jit(solution)/shard_map/while/body/eval_jaxpr/gik,gkf->gif/dot_general | solution.py:32
  98.5 14.5 %scatter_fusion = f32[32,128,256]{2,1,0:T(8,128)} fusion(f32[32,128,256]{2,1,0:T(8,128)} %get-tuple-element.205, s32[46]{0:T(128)S(1)} %get-tuple-element.191, f32[46,128,256]{2,1,0:T(8,128)} %fusion.13), kind=kCustom, calls=%fused_computation.1.clone.1 | custom fusion | flops 1507328 | bytes 18088120 | tf_op jit(solution)/shard_map/while/body/eval_jaxpr/scatter-add | solution.py:33
  113.0 0.7 add_compare_fusion.2
  113.6 0.1 compare_select_fusion.3
  113.7 2.9 gather_fusion
  116.6 5.0 %fusion.13 = f32[46,128,256]{2,1,0:T(8,128)} fusion(bf16[46,128,256]{2,1,0:T(8,128)(2,1)S(1)} %gather_fusion, bf16[368,128,128]{2,1,0:T(8,128)(2,1)} %get-tuple-element.219, s32[]{:T(128)S(6)} %select_n.40, pred[46]{0:T(512)(128)(4,1)S(1)} %add_compare_fusion.2), kind=kOutput, calls=%fused_computation.2.clone.1 | convolution fusion | flops 386629632 | bytes 10551346 | tf_op jit(solution)/shard_map/while/body/eval_jaxpr/gik,gkf->gif/dot_general | solution.py:32
  121.6 14.5 %scatter_fusion = f32[32,128,256]{2,1,0:T(8,128)} fusion(f32[32,128,256]{2,1,0:T(8,128)} %get-tuple-element.205, s32[46]{0:T(128)S(1)} %get-tuple-element.191, f32[46,128,256]{2,1,0:T(8,128)} %fusion.13), kind=kCustom, calls=%fused_computation.1.clone.1 | custom fusion | flops 1507328 | bytes 18088120 | tf_op jit(solution)/shard_map/while/body/eval_jaxpr/scatter-add | solution.py:33
  136.1 0.7 add_compare_fusion.2
  136.7 0.1 compare_select_fusion.3
  136.8 2.9 gather_fusion
  139.8 5.0 %fusion.13 = f32[46,128,256]{2,1,0:T(8,128)} fusion(bf16[46,128,256]{2,1,0:T(8,128)(2,1)S(1)} %gather_fusion, bf16[368,128,128]{2,1,0:T(8,128)(2,1)} %get-tuple-element.219, s32[]{:T(128)S(6)} %select_n.40, pred[46]{0:T(512)(128)(4,1)S(1)} %add_compare_fusion.2), kind=kOutput, calls=%fused_computation.2.clone.1 | convolution fusion | flops 386629632 | bytes 10551346 | tf_op jit(solution)/shard_map/while/body/eval_jaxpr/gik,gkf->gif/dot_general | solution.py:32
  144.7 14.3 %scatter_fusion = f32[32,128,256]{2,1,0:T(8,128)} fusion(f32[32,128,256]{2,1,0:T(8,128)} %get-tuple-element.205, s32[46]{0:T(128)S(1)} %get-tuple-element.191, f32[46,128,256]{2,1,0:T(8,128)} %fusion.13), kind=kCustom, calls=%fused_computation.1.clone.1 | custom fusion | flops 1507328 | bytes 18088120 | tf_op jit(solution)/shard_map/while/body/eval_jaxpr/scatter-add | solution.py:33
  159.0 0.7 add_compare_fusion.2
  159.7 0.1 compare_select_fusion.3
  159.8 2.9 gather_fusion
  162.7 5.0 %fusion.13 = f32[46,128,256]{2,1,0:T(8,128)} fusion(bf16[46,128,256]{2,1,0:T(8,128)(2,1)S(1)} %gather_fusion, bf16[368,128,128]{2,1,0:T(8,128)(2,1)} %get-tuple-element.219, s32[]{:T(128)S(6)} %select_n.40, pred[46]{0:T(512)(128)(4,1)S(1)} %add_compare_fusion.2), kind=kOutput, calls=%fused_computation.2.clone.1 | convolution fusion | flops 386629632 | bytes 10551346 | tf_op jit(solution)/shard_map/while/body/eval_jaxpr/gik,gkf->gif/dot_general | solution.py:32
  167.7 14.6 %scatter_fusion = f32[32,128,256]{2,1,0:T(8,128)} fusion(f32[32,128,256]{2,1,0:T(8,128)} %get-tuple-element.205, s32[46]{0:T(128)S(1)} %get-tuple-element.191, f32[46,128,256]{2,1,0:T(8,128)} %fusion.13), kind=kCustom, calls=%fused_computation.1.clone.1 | custom fusion | flops 1507328 | bytes 18088120 | tf_op jit(solution)/shard_map/while/body/eval_jaxpr/scatter-add | solution.py:33
  182.3 0.7 add_compare_fusion.2
  182.9 0.1 compare_select_fusion.3
  183.0 2.9 gather_fusion
  186.0 5.0 %fusion.13 = f32[46,128,256]{2,1,0:T(8,128)} fusion(bf16[46,128,256]{2,1,0:T(8,128)(2,1)S(1)} %gather_fusion, bf16[368,128,128]{2,1,0:T(8,128)(2,1)} %get-tuple-element.219, s32[]{:T(128)S(6)} %select_n.40, pred[46]{0:T(512)(128)(4,1)S(1)} %add_compare_fusion.2), kind=kOutput, calls=%fused_computation.2.clone.1 | convolution fusion | flops 386629632 | bytes 10551346 | tf_op jit(solution)/shard_map/while/body/eval_jaxpr/gik,gkf->gif/dot_general | solution.py:32
  190.9 14.6 %scatter_fusion = f32[32,128,256]{2,1,0:T(8,128)} fusion(f32[32,128,256]{2,1,0:T(8,128)} %get-tuple-element.205, s32[46]{0:T(128)S(1)} %get-tuple-element.191, f32[46,128,256]{2,1,0:T(8,128)} %fusion.13), kind=kCustom, calls=%fused_computation.1.clone.1 | custom fusion | flops 1507328 | bytes 18088120 | tf_op jit(solution)/shard_map/while/body/eval_jaxpr/scatter-add | solution.py:33
  205.6 0.7 add_compare_fusion.2
  206.2 0.1 compare_select_fusion.3
  206.3 2.9 gather_fusion
  209.2 5.0 %fusion.13 = f32[46,128,256]{2,1,0:T(8,128)} fusion(bf16[46,128,256]{2,1,0:T(8,128)(2,1)S(1)} %gather_fusion, bf16[368,128,128]{2,1,0:T(8,128)(2,1)} %get-tuple-element.219, s32[]{:T(128)S(6)} %select_n.40, pred[46]{0:T(512)(128)(4,1)S(1)} %add_compare_fusion.2), kind=kOutput, calls=%fused_computation.2.clone.1 | convolution fusion | flops 386629632 | bytes 10551346 | tf_op jit(solution)/shard_map/while/body/eval_jaxpr/gik,gkf->gif/dot_general | solution.py:32
  214.2 14.6 %scatter_fusion = f32[32,128,256]{2,1,0:T(8,128)} fusion(f32[32,128,256]{2,1,0:T(8,128)} %get-tuple-element.205, s32[46]{0:T(128)S(1)} %get-tuple-element.191, f32[46,128,256]{2,1,0:T(8,128)} %fusion.13), kind=kCustom, calls=%fused_computation.1.clone.1 | custom fusion | flops 1507328 | bytes 18088120 | tf_op jit(solution)/shard_map/while/body/eval_jaxpr/scatter-add | solution.py:33
  228.8 0.7 add_compare_fusion.2
  229.5 0.1 compare_select_fusion.3
  229.6 2.9 gather_fusion
  232.5 5.0 %fusion.13 = f32[46,128,256]{2,1,0:T(8,128)} fusion(bf16[46,128,256]{2,1,0:T(8,128)(2,1)S(1)} %gather_fusion, bf16[368,128,128]{2,1,0:T(8,128)(2,1)} %get-tuple-element.219, s32[]{:T(128)S(6)} %select_n.40, pred[46]{0:T(512)(128)(4,1)S(1)} %add_compare_fusion.2), kind=kOutput, calls=%fused_computation.2.clone.1 | convolution fusion | flops 386629632 | bytes 10551346 | tf_op jit(solution)/shard_map/while/body/eval_jaxpr/gik,gkf->gif/dot_general | solution.py:32
  237.5 14.6 %scatter_fusion = f32[32,128,256]{2,1,0:T(8,128)} fusion(f32[32,128,256]{2,1,0:T(8,128)} %get-tuple-element.205, s32[46]{0:T(128)S(1)} %get-tuple-element.191, f32[46,128,256]{2,1,0:T(8,128)} %fusion.13), kind=kCustom, calls=%fused_computation.1.clone.1 | custom fusion | flops 1507328 | bytes 18088120 | tf_op jit(solution)/shard_map/while/body/eval_jaxpr/scatter-add | solution.py:33
  252.0 3.8 %convert_element_type.6 = bf16[32,128,256]{2,1,0:T(8,128)(2,1)} convert(f32[32,128,256]{2,1,0:T(8,128)} %get-tuple-element.129) | non-fusion elementwise | flops 1048576 | bytes 6291456 | tf_op jit(solution)/shard_map/convert_element_type | solution.py:39
  255.9 0.0 reduce-scatter.2.cloned.1.call-update
  255.9 43.6 %reduce-scatter.2.cloned.1.call-done = bf16[1024,256]{1,0:T(8,128)(2,1)} async-done(((bf16[4096,256]{1,0:T(8,128)(2,1)}), bf16[1024,256]{1,0:T(8,128)(2,1)}) %reduce-scatter.2.cloned.1.call-update) | async-done | bytes 524304 | tf_op jit(solution)/shard_map/reduce_scatter | solution.py:38
  (10 shorter events, 0.1 us)
Async XLA Ops:
  9.8 5.4 %copy-start = (s32[1,1,368]{2,1,0:T(1,128)S(1)}, s32[1,1,368]{2,1,0:T(1,128)}, u32[]{:S(2)}) copy-start(s32[1,1,368]{2,1,0:T(1,128)} %param.8) | copy-start | bytes 4420
  9.8 5.4 %copy-start.1 = (s32[1,1,368]{2,1,0:T(1,128)S(1)}, s32[1,1,368]{2,1,0:T(1,128)}, u32[]{:S(2)}) copy-start(s32[1,1,368]{2,1,0:T(1,128)} %param.9) | copy-start | bytes 4420
  9.8 54.5 %all-to-all-start = ((bf16[8,1024,256]{2,1,0:T(8,128)(2,1)}), bf16[8,1024,256]{2,1,0:T(8,128)(2,1)}, u32[]{:S(2)}, u32[]{:S(2)}) async-start(bf16[8,1024,256]{2,1,0:T(8,128)(2,1)} %stack.2), calls=%async_computation | async-start | bytes 8388608 | tf_op jit(solution)/shard_map/all_to_all | solution.py:14
  15.1 284.4 %reduce-scatter.2.cloned.1.call-start = ((), (), s32[]{:S(2)}) async-start(), calls=%async_computation.2 | async-start | bytes 2621440 | tf_op jit(solution)/shard_map/reduce_scatter | solution.py:38
Sparse Core Ops, SparseCore 0:
  256.0 43.4 reduce-scatter.1
